TPU v7x, 256 devices: a whole 4x4x8 slice. The times are simulated.
256 devices in a mesh: dp: 8 (over x, core), rows: 32 (over y, z).
Axes of the slice: x: 4, y: 4, z: 8, core: 2. Of those that a mesh axis runs over, the one named last changes fastest.
Arguments:
- grads: bfloat16 [2, 4096, 14336], P(None, 'rows', 'dp'), may hold values from -64 to 64
- basis: bfloat16 [2, 4096, 512], P(None, 'rows'), may hold values from -0.09375 to 0.09375
- moment1: float32 [2, 512, 14336], P(None, 'rows', 'dp'), may hold values from -0.3 to 0.3
- moment2: float32 [2, 512, 14336], P(None, 'rows', 'dp'), may hold values from 0.001 to 0.03
- weights: bfloat16 [2, 4096, 14336], P(None, 'rows', 'dp'), may hold values from -0.09375 to 0.09375
Outputs:
- new_weights: bfloat16 [2, 4096, 14336], P(None, 'rows')
- new_moment1: float32 [2, 512, 14336], P(None, 'rows', 'dp')
- new_moment2: float32 [2, 512, 14336], P(None, 'rows', 'dp')
All inputs are finite; a program needn't handle non-finite values.
Results may differ from a plain program's by a relative error of at most 0.00115.
The roundings to bfloat16 on the way count: a program that leaves them out, or rounds other values in their place, can miss the bound.
Values may be sent and summed in bfloat16 or wider, within the bound.
No kernel may reach another device: no remote copies, remote signals or barrier semaphores. Data moves between devices by JAX's collectives and lax.ppermute only.
A program may use at most 64 MiB of HBM per device.

v0:
```python
import math
import jax
import jax.numpy as jnp
from jax import lax
from jax.sharding import Mesh
from jax.sharding import PartitionSpec as P

D = 4096
FF = 14336
MATS = 2
STEP = 10
ROWS = ("rows_0", "rows_1")


def sum_by_axis(x, axes, dim):
    for axis in axes:
        x = lax.psum_scatter(x, axis, scatter_dimension=dim, tiled=True)
    return x


def laid_out(tiles, dim):
    tiles = jnp.moveaxis(tiles, 0, dim)
    shape = tiles.shape
    return tiles.reshape(*shape[:dim], shape[dim] * shape[dim + 1], *shape[dim + 2 :])


def gather_in_order(x, axes, turns):
    tiles = x[None]
    for k in turns:
        tiles = lax.all_gather(tiles, axes[k], axis=0, tiled=True)
    carried = [lax.axis_size(axes[k]) for k in reversed(turns)]
    tiles = tiles.reshape(*carried, *x.shape)
    turned = sorted(range(len(turns)), key=lambda place: turns[len(turns) - 1 - place])
    return tiles.transpose(*turned, *range(len(turns), tiles.ndim)).reshape(-1, *x.shape)


def whole_of(x, axes, turns, dim):
    return laid_out(gather_in_order(x, axes, turns), dim)


def moment_step(projected, moment1, moment2, total):
    limit = 1.0 * math.sqrt(MATS * D * FF)
    scale = limit / jnp.maximum(jnp.sqrt(total), limit)
    scaled = scale * projected
    first = 0.9 * moment1 + 0.1 * scaled
    second = 0.999 * moment2 + 0.001 * scaled * scaled
    first_bias_correction = 1.0 - 0.9**STEP
    second_fix = 1.0 - 0.999**STEP
    low_rank_update = (
        first / first_bias_correction / (jnp.sqrt(second / second_fix) + 1e-08)
    ).astype(jnp.bfloat16)
    return (first, second, low_rank_update)


def local(grads, basis, moment1, moment2, weights):
    grad_wide = grads.astype(jnp.float32)
    own_squares = jnp.sum(grad_wide * grad_wide)
    partial_norm_value = jnp.einsum(
        "yka,ykx->yax", basis, grads, preferred_element_type=jnp.float32
    )
    column_square_sum = jnp.full((lax.axis_size(ROWS),), own_squares, jnp.float32)
    projected, group_squares = (
        sum_by_axis(partial_norm_value, ROWS, 1),
        sum_by_axis(column_square_sum, ROWS, 0),
    )
    total = lax.psum(group_squares[0], "dp")
    first, second, low_rank_update = moment_step(projected, moment1, moment2, total)
    projected_back = jnp.einsum(
        "auw,awl->aul",
        basis,
        whole_of(low_rank_update, ROWS, (0, 1), 1),
        preferred_element_type=jnp.float32,
    )
    fresh = (weights.astype(jnp.float32) - 0.5 * projected_back).astype(jnp.bfloat16)
    whole_rows = lax.all_gather(fresh, "dp", axis=2, tiled=True)
    return (whole_rows, first, second)


def solution(mesh):
    finer = Mesh(mesh.devices.reshape(mesh.shape["dp"], 4, 8), ("dp", "rows_0", "rows_1"))
    in_specs = (
        P(None, ROWS, "dp"),
        P(None, ROWS, None),
        P(None, ROWS, "dp"),
        P(None, ROWS, "dp"),
        P(None, ROWS, "dp"),
    )
    out_specs = (P(None, ROWS, None), P(None, ROWS, "dp"), P(None, ROWS, "dp"))
    return jax.shard_map(local, mesh=finer, in_specs=in_specs, out_specs=out_specs, check_vma=False)
```

profile of v0, /device:TPU:1, one launch (start us, length us, event | category | flops | bytes accessed | tf_op | source)
XLA Modules:
  0.0 268.7 jit_solution(6423044746754964495)
XLA Ops:
  7.2 0.0 reduce-scatter.3.cloned.1.call-start
  7.2 0.9 copy-done
  8.1 5.4 %fusion.5 = f32[2,512,1792]{2,1,0:T(8,128)} fusion(bf16[2,128,512]{2,1,0:T(8,128)(2,1)S(1)} %copy-done, bf16[2,128,1792]{2,1,0:T(8,128)(2,1)} %param.5), kind=kOutput, calls=%fused_computation.9 | convolution fusion | flops 469762048 | bytes 8519680 | tf_op jit(solution)/shard_map/yka,ykx->yax/dot_general | solution.py:58
  13.6 0.0 reduce-scatter.5.cloned.1.call-start
  13.6 78.9 %reduce-scatter.3.cloned.1.call-done = f32[2,128,1792]{2,1,0:T(8,128)} async-done(((f32[2,512,1792]{2,1,0:T(8,128)}), f32[2,128,1792]{2,1,0:T(8,128)}) %reduce-scatter.3.cloned.1.call-update) | async-done | bytes 1835024 | tf_op jit(solution)/shard_map/reduce_scatter | solution.py:17
  92.6 0.0 all-gather.4.cloned.1.call-start
  92.6 0.6 dynamic-slice
  93.9 1.1 multiply_reduce_fusion
  95.0 0.6 broadcast_in_dim.6
  95.6 6.6 %all-reduce = f32[32]{0:T(128)S(1)} all-reduce(f32[32]{0:T(128)S(1)} %broadcast_in_dim.6), channel_id=3, replica_groups=mesh['dp'=8,'rows_0'=4,'rows_1'=8] {'rows_0'}, use_global_device_ids=true, to_apply=%region_1.0.clone | all-reduce | flops 32 | bytes 256
  102.2 0.1 dynamic-slice.1
  102.2 14.4 %all-reduce.1 = f32[8]{0:T(128)S(1)} all-reduce(f32[8]{0:T(128)S(1)} %dynamic-slice.1), channel_id=4, replica_groups=mesh['dp'=8,'rows_0'=4,'rows_1'=8] {'rows_1'}, use_global_device_ids=true, to_apply=%region_2.0.clone | all-reduce | flops 8 | bytes 64
  116.6 0.6 dynamic-slice.2
  117.2 1.2 dynamic-slice.3
  118.5 18.6 %psum.7 = f32[]{:T(128)} all-reduce(f32[]{:T(128)} %bitcast), channel_id=1, replica_groups=mesh['dp'=8,'rows_0'=4,'rows_1'=8] {'dp'}, use_global_device_ids=true, to_apply=%region_3.0 | all-reduce | flops 1 | bytes 8 | tf_op jit(solution)/shard_map/psum | solution.py:66
  137.9 1.8 divide_convert_fusion
  139.7 10.5 %all-gather = bf16[8,16,1792]{2,1,0:T(8,128)(2,1)} all-gather(bf16[2,16,1792]{2,1,0:T(8,128)(2,1)S(1)} %get-tuple-element.12), channel_id=2, replica_groups=mesh['dp'=8,'rows_0'=4,'rows_1'=8] {'rows_0'}, dimensions={0}, use_global_device_ids=true | all-gather | bytes 573440 | tf_op jit(solution)/shard_map/all_gather | solution.py:30
  150.2 0.0 all-gather.6.cloned.1.call-start
  150.3 0.6 copy.17
  150.9 49.1 %all-gather.4.cloned.1.call-done = bf16[32,2,16,1792]{3,2,1,0:T(8,128)(2,1)} async-done(((bf16[4,2,16,1792]{3,2,1,0:T(8,128)(2,1)}), bf16[32,2,16,1792]{3,2,1,0:T(8,128)(2,1)}) %all-gather.4.cloned.1.call-update) | async-done | bytes 3670032 | tf_op jit(solution)/shard_map/all_gather | solution.py:30
  200.0 2.3 copy.19
  202.4 2.5 fusion.2
  204.9 47.1 %all-gather.6.cloned.1.call-done = bf16[2,128,14336]{1,2,0:T(8,128)(2,1)} async-done(((bf16[2,128,1792]{1,2,0:T(8,128)(2,1)}), bf16[2,128,14336]{1,2,0:T(8,128)(2,1)}) %all-gather.6.cloned.1.call-update) | async-done | bytes 7340048 | tf_op jit(solution)/shard_map/all_gather | solution.py:75
  252.0 10.1 %copy.21 = bf16[2,128,14336]{2,1,0:T(8,128)(2,1)} copy(bf16[2,128,14336]{1,2,0:T(8,128)(2,1)} %all-gather.6.cloned.1.call-done) | data formatting | bytes 14680064
  (18 shorter events, 0.1 us)
Async XLA Ops:
  7.2 1.0 copy-start
  7.2 85.4 %reduce-scatter.3.cloned.1.call-start = ((), (), s32[]{:S(2)}) async-start(), calls=%async_computation.2 | async-start | bytes 9175040 | tf_op jit(solution)/shard_map/reduce_scatter | solution.py:17
  13.5 79.1 %copy-start.6 = (u32[256]{0:T(256)S(1)}, u32[256]{0:T(256)}, u32[]{:S(2)}) copy-start(u32[256]{0:T(256)} %constant.26) | copy-start | bytes 3076
  13.5 80.4 %copy-start.1 = (bf16[2,128,1792]{2,1,0:T(8,128)(2,1)S(1)}, bf16[2,128,1792]{2,1,0:T(8,128)(2,1)}, u32[]{:S(2)}) copy-start(bf16[2,128,1792]{2,1,0:T(8,128)(2,1)} %param.5) | copy-start | bytes 2752516
  13.5 103.1 %copy-start.5 = (u32[256]{0:T(256)S(1)}, u32[256]{0:T(256)}, u32[]{:S(2)}) copy-start(u32[256]{0:T(256)} %constant.30) | copy-start | bytes 3076
  13.5 124.3 %copy-start.3 = (f32[2,16,1792]{2,1,0:T(8,128)S(1)}, f32[2,16,1792]{2,1,0:T(8,128)}, u32[]{:S(2)}) copy-start(f32[2,16,1792]{2,1,0:T(8,128)} %param.7) | copy-start | bytes 688132
  13.5 124.4 %copy-start.4 = (f32[2,16,1792]{2,1,0:T(8,128)S(1)}, f32[2,16,1792]{2,1,0:T(8,128)}, u32[]{:S(2)}) copy-start(f32[2,16,1792]{2,1,0:T(8,128)} %param.8) | copy-start | bytes 688132
  13.6 136.7 %copy-start.2 = (bf16[2,128,1792]{2,1,0:T(8,128)(2,1)S(1)}, bf16[2,128,1792]{2,1,0:T(8,128)(2,1)}, u32[]{:S(2)}) copy-start(bf16[2,128,1792]{2,1,0:T(8,128)(2,1)} %param.9) | copy-start | bytes 2752516
  13.6 124.3 %reduce-scatter.5.cloned.1.call-start = ((), (), s32[]{:S(2)}) async-start(), calls=%async_computation.3 | async-start | bytes 2064384 | tf_op jit(solution)/shard_map/reduce_scatter | solution.py:17
  92.6 107.5 %all-gather.4.cloned.1.call-start = ((), (), s32[]{:S(2)}) async-start(), calls=%async_computation.4 | async-start | bytes 4128768 | tf_op jit(solution)/shard_map/all_gather | solution.py:30
  150.2 101.8 %all-gather.6.cloned.1.call-start = ((), (), s32[]{:S(2)}) async-start(), calls=%async_computation.5 | async-start | bytes 8257536 | tf_op jit(solution)/shard_map/all_gather | solution.py:75
Sparse Core Ops, SparseCore 0:
  13.7 78.8 reduce-scatter.2
  95.1 37.1 reduce-scatter.4
  150.4 49.6 all-gather.3
  205.0 46.9 all-gather.5
where the time goes:
time: 269 us
  waiting for transfers between devices  175 us (65%)
  blocking collectives  50.1 us (19%)
  local copies, waits for them, and re-layouts  17.1 us (6%)
  between operations  15.3 us (6%)
  matrix products  7.89 us (3%)
  other arithmetic  2.92 us (1%)
    reduce_scatter x2, waiting for transfers between devices, sum_by_axis(): x = lax.psum_scatter(x, axis, scatter_dimension=dim, tiled=True)  79 us
    all_gather x1, waiting for transfers between devices, gather_in_order(): tiles = lax.all_gather(tiles, axes[k], axis=0, tiled=True)  49.1 us
    all_gather x1, waiting for transfers between devices, local(): whole_rows = lax.all_gather(fresh, 'dp', axis=2, tiled=True)  47.1 us
    unnamed x2, blocking collectives  20.9 us
    psum x1, blocking collectives, local(): total = lax.psum(group_squares[0], 'dp')  18.6 us
    unnamed x20, local copies, waits for them, and re-layouts  14.2 us
    all_gather x1, blocking collectives, gather_in_order(): tiles = lax.all_gather(tiles, axes[k], axis=0, tiled=True)  10.5 us
    dot_general x1, matrix products, local(): jnp.einsum('yka,ykx->yax', basis, grads, preferred_element_type=jnp.float32)  5.38 us
  transfers between devices with their start and end apart: 4, of which 3 were waited for; matrix products, arithmetic and copies ran while one was open for 2% of the time, Pallas kernels for 0%

commit v1 on v0

--- a/solution.py
+++ b/solution.py
@@ -72,7 +72,9 @@
         preferred_element_type=jnp.float32,
     )
     fresh = (weights.astype(jnp.float32) - 0.5 * projected_back).astype(jnp.bfloat16)
-    whole_rows = lax.all_gather(fresh, "dp", axis=2, tiled=True)
+    whole_rows = jnp.concatenate(
+        lax.all_to_all(jnp.stack([fresh] * lax.axis_size("dp")), "dp", 0, 0), axis=2
+    )
     return (whole_rows, first, second)
 
 

time: 269 us -> 320 us (1.19)
  blocking collectives: 50.1 us -> 137 us
  waiting for transfers between devices: 175 us -> 128 us
  local copies, waits for them, and re-layouts: 17.1 us -> 28.4 us
    all_to_all x0 -> x1, blocking collectives: none -> 87.3 us  [local(): lax.all_to_all(jnp.stack([fresh] * lax.axis_size('dp')), 'dp', 0, 0)]
    all_gather x1 -> x0, waiting for transfers between devices: 47.1 us -> none  [local(): whole_rows = lax.all_gather(fresh, 'dp', axis=2, tiled=True)]
    all_to_all x0 -> x1, local copies, waits for them, and re-layouts: none -> 10 us  [local(): lax.all_to_all(jnp.stack([fresh] * lax.axis_size('dp')), 'dp', 0, 0)]
  transfers between devices with their start and end apart: 4 -> 3, of which waited for: 3 -> 2; matrix products, arithmetic and copies ran while one was open for 2% -> 2% of each run, Pallas kernels for 0% -> 0%
where the time goes in v1:
time: 320 us; the launch traced here: 319 us
  blocking collectives  137 us (43%)
  waiting for transfers between devices  128 us (40%)
  local copies, waits for them, and re-layouts  28.4 us (9%)
  between operations  15.3 us (5%)
  matrix products  6.96 us (2%)
    all_to_all x1, blocking collectives, local(): lax.all_to_all(jnp.stack([fresh] * lax.axis_size('dp')), 'dp', 0, 0)  87.3 us
    reduce_scatter x2, waiting for transfers between devices, sum_by_axis(): x = lax.psum_scatter(x, axis, scatter_dimension=dim, tiled=True)  79 us
    all_gather x1, waiting for transfers between devices, gather_in_order(): tiles = lax.all_gather(tiles, axes[k], axis=0, tiled=True)  49.2 us
    unnamed x2, blocking collectives  20.9 us
    psum x1, blocking collectives, local(): total = lax.psum(group_squares[0], 'dp')  18.6 us
    unnamed x20, local copies, waits for them, and re-layouts  14.2 us
    all_gather x1, blocking collectives, gather_in_order(): tiles = lax.all_gather(tiles, axes[k], axis=0, tiled=True)  10.5 us
    all_to_all x1, local copies, waits for them, and re-layouts, local(): lax.all_to_all(jnp.stack([fresh] * lax.axis_size('dp')), 'dp', 0, 0)  10 us
  transfers between devices with their start and end apart: 3, of which 2 were waited for; matrix products, arithmetic and copies ran while one was open for 2% of the time, Pallas kernels for 0%

profile of v1, /device:TPU:1, one launch (start us, length us, event | category | flops | bytes accessed | tf_op | source)
XLA Modules:
  0.0 319.3 jit_solution(3272971600563607807)
XLA Ops:
  7.2 0.9 copy-done
  8.1 5.4 %fusion.5 = f32[2,512,1792]{2,1,0:T(8,128)} fusion(bf16[2,128,512]{2,1,0:T(8,128)(2,1)S(1)} %copy-done, bf16[2,128,1792]{2,1,0:T(8,128)(2,1)} %param.5), kind=kOutput, calls=%fused_computation.9 | convolution fusion | flops 469762048 | bytes 8519680 | tf_op jit(solution)/shard_map/yka,ykx->yax/dot_general | solution.py:58
  13.6 0.0 reduce-scatter.5.cloned.1.call-start
  13.6 78.9 %reduce-scatter.3.cloned.1.call-done = f32[2,128,1792]{2,1,0:T(8,128)} async-done(((f32[2,512,1792]{2,1,0:T(8,128)}), f32[2,128,1792]{2,1,0:T(8,128)}) %reduce-scatter.3.cloned.1.call-update) | async-done | bytes 1835024 | tf_op jit(solution)/shard_map/reduce_scatter | solution.py:17
  92.6 0.6 dynamic-slice
  93.9 1.1 multiply_reduce_fusion
  95.0 0.6 broadcast_in_dim.6
  95.6 6.6 %all-reduce = f32[32]{0:T(128)S(1)} all-reduce(f32[32]{0:T(128)S(1)} %broadcast_in_dim.6), channel_id=3, replica_groups=mesh['dp'=8,'rows_0'=4,'rows_1'=8] {'rows_0'}, use_global_device_ids=true, to_apply=%region_1.0.clone | all-reduce | flops 32 | bytes 256
  102.2 0.1 dynamic-slice.1
  102.2 14.4 %all-reduce.1 = f32[8]{0:T(128)S(1)} all-reduce(f32[8]{0:T(128)S(1)} %dynamic-slice.1), channel_id=4, replica_groups=mesh['dp'=8,'rows_0'=4,'rows_1'=8] {'rows_1'}, use_global_device_ids=true, to_apply=%region_2.0.clone | all-reduce | flops 8 | bytes 64
  116.6 0.6 dynamic-slice.2
  117.2 1.2 dynamic-slice.3
  118.5 18.6 %psum.7 = f32[]{:T(128)} all-reduce(f32[]{:T(128)} %bitcast), channel_id=1, replica_groups=mesh['dp'=8,'rows_0'=4,'rows_1'=8] {'dp'}, use_global_device_ids=true, to_apply=%region_3.0 | all-reduce | flops 1 | bytes 8 | tf_op jit(solution)/shard_map/psum | solution.py:66
  137.9 1.8 divide_convert_fusion
  139.7 10.5 %all-gather = bf16[8,16,1792]{2,1,0:T(8,128)(2,1)} all-gather(bf16[2,16,1792]{2,1,0:T(8,128)(2,1)S(1)} %get-tuple-element.6), channel_id=2, replica_groups=mesh['dp'=8,'rows_0'=4,'rows_1'=8] {'rows_0'}, dimensions={0}, use_global_device_ids=true | all-gather | bytes 573440 | tf_op jit(solution)/shard_map/all_gather | solution.py:30
  150.3 0.6 copy.22
  150.9 49.2 %all-gather.3.cloned.1.call-done = bf16[32,2,16,1792]{3,2,1,0:T(8,128)(2,1)} async-done(((bf16[4,2,16,1792]{3,2,1,0:T(8,128)(2,1)}), bf16[32,2,16,1792]{3,2,1,0:T(8,128)(2,1)}) %all-gather.3.cloned.1.call-update) | async-done | bytes 3670032 | tf_op jit(solution)/shard_map/all_gather | solution.py:30
  200.0 2.3 copy.24
  202.4 1.6 fusion.2
  204.0 0.5 copy.26
  204.5 0.7 stack.2
  205.2 87.3 %all_to_all.5 = bf16[8,2,128,1792]{3,2,1,0:T(8,128)(2,1)} all-to-all(bf16[8,2,128,1792]{3,2,1,0:T(8,128)(2,1)S(1)} %stack.2), channel_id=1, replica_groups=mesh['dp'=8,'rows_0'=4,'rows_1'=8] {'dp'}, dimensions={0} | all-to-all | bytes 14680064 | tf_op jit(solution)/shard_map/all_to_all | solution.py:76
  292.6 10.0 %copy.27 = bf16[8,2,128,1792]{2,3,0,1:T(8,128)(2,1)} copy(bf16[8,2,128,1792]{3,2,1,0:T(8,128)(2,1)} %all_to_all.5) | data formatting | bytes 14680064 | tf_op jit(solution)/shard_map/all_to_all | solution.py:76
  302.6 10.1 %copy.28 = bf16[2,128,14336]{2,1,0:T(8,128)(2,1)} copy(bf16[2,128,14336]{1,2,0:T(8,128)(2,1)} %bitcast.25) | data formatting | bytes 14680064
  (19 shorter events, 0.2 us)
Async XLA Ops:
  7.2 1.0 copy-start
  7.2 85.4 %reduce-scatter.3.cloned.1.call-start = ((), (), s32[]{:S(2)}) async-start(), calls=%async_computation.3 | async-start | bytes 9175040 | tf_op jit(solution)/shard_map/reduce_scatter | solution.py:17
  13.5 79.1 %copy-start.6 = (u32[256]{0:T(256)S(1)}, u32[256]{0:T(256)}, u32[]{:S(2)}) copy-start(u32[256]{0:T(256)} %constant.26) | copy-start | bytes 3076
  13.5 80.4 %copy-start.1 = (bf16[2,128,1792]{2,1,0:T(8,128)(2,1)S(1)}, bf16[2,128,1792]{2,1,0:T(8,128)(2,1)}, u32[]{:S(2)}) copy-start(bf16[2,128,1792]{2,1,0:T(8,128)(2,1)} %param.5) | copy-start | bytes 2752516
  13.5 103.1 %copy-start.5 = (u32[256]{0:T(256)S(1)}, u32[256]{0:T(256)}, u32[]{:S(2)}) copy-start(u32[256]{0:T(256)} %constant.30) | copy-start | bytes 3076
  13.5 124.3 %copy-start.3 = (f32[2,16,1792]{2,1,0:T(8,128)S(1)}, f32[2,16,1792]{2,1,0:T(8,128)}, u32[]{:S(2)}) copy-start(f32[2,16,1792]{2,1,0:T(8,128)} %param.7) | copy-start | bytes 688132
  13.5 124.4 %copy-start.4 = (f32[2,16,1792]{2,1,0:T(8,128)S(1)}, f32[2,16,1792]{2,1,0:T(8,128)}, u32[]{:S(2)}) copy-start(f32[2,16,1792]{2,1,0:T(8,128)} %param.8) | copy-start | bytes 688132
  13.6 136.7 %copy-start.2 = (bf16[2,128,1792]{2,1,0:T(8,128)(2,1)S(1)}, bf16[2,128,1792]{2,1,0:T(8,128)(2,1)}, u32[]{:S(2)}) copy-start(bf16[2,128,1792]{2,1,0:T(8,128)(2,1)} %param.9) | copy-start | bytes 2752516
  13.6 124.3 %reduce-scatter.5.cloned.1.call-start = ((), (), s32[]{:S(2)}) async-start(), calls=%async_computation.4 | async-start | bytes 2064384 | tf_op jit(solution)/shard_map/reduce_scatter | solution.py:17
  92.6 107.5 %all-gather.3.cloned.1.call-start = ((), (), s32[]{:S(2)}) async-start(), calls=%async_computation.5 | async-start | bytes 4128768 | tf_op jit(solution)/shard_map/all_gather | solution.py:30
Sparse Core Ops, SparseCore 0:
  13.7 78.8 reduce-scatter.2
  95.1 37.1 reduce-scatter.4
  150.4 49.6 all-gather.2
